TPU v7x, 32 devices: a whole 2x2x4 slice. The times are simulated.
32 devices in a mesh: space: 16 (over z, y, x), rep: 2 (over core).
Axes of the slice: x: 2, y: 2, z: 4, core: 2. Of those that a mesh axis runs over, the one named last changes fastest.
Arguments:
- halo_rows: bfloat16 [4, 2048, 256], P(None, 'space', 'rep'), may hold values from -6 to 6
- unmatched: int32 [4, 2048], P(None, 'space'), may hold values 0 or 1
- owner_id: int32 [4, 2048, 1], P(None, 'space'), may hold values from 0 to 15; in each aligned block of 128 rows (0 to 127, 128 to 255, ..., all dimensions but the last counted through in order) at most 16 rows name the same one
- cand_index: int32 [4, 2048, 16], P(None, 'space'), may hold values from 0 to 511
- lengths: int32 [4, 2048], P(None, 'space'), may hold values from 1 to 16
- choice_index: int32 [4, 2048], P(None, 'space'), may hold values from 0 to 15, as said below
- desc_rows: bfloat16 [4, 8192, 256], P(None, 'space', 'rep'), may hold values from -6 to 6
Outputs:
- phantom: bfloat16 [4, 2048, 256], P(None, 'space', 'rep')
- best_merit: bfloat16 [4, 2048], P(None, 'space')
Inputs may be any that keep to these rules, and one draw needn't show every extreme that they name: `owner_id`: in each aligned block of 128 halos (one region in one snapshot) no owner is named by more than 16 halos, a bound that some block reaches. `choice_index`: less than the halo's length.
All inputs are finite; a program needn't handle non-finite values. No bound on the sum of `unmatched` on one device may be relied on, other than what follows from the above.
Results may differ from a plain program's by a relative error of at most 0.001.
Values may be sent and summed in bfloat16 or wider, within the bound.
A program may use at most 64 MiB of HBM per device.

v0:
```python
import functools
import math

import jax
import jax.numpy as jnp
from jax import lax
from jax.experimental import pallas as pl
from jax.experimental.pallas import tpu as pltpu
from jax.sharding import PartitionSpec as P

MESH = pl.DeviceIdType.MESH
F32 = jnp.float32
BF16 = jnp.bfloat16
NEG = -1e30
GROUP = 32
NT = (((1,), (1,)), ((), ()))
TN = (((0,), (0,)), ((), ()))


def iota(shape, dim):
    return lax.broadcasted_iota(jnp.int32, shape, dim)


def dot(a, b):
    return jnp.dot(a, b, preferred_element_type=F32)


def hot(mask):
    return jnp.where(mask, 1.0, 0.0).astype(BF16)


def code(index, cands):
    return index - cands // 2 + jnp.where(index >= cands // 2, 1, 0)


def kernel(
    n, slots, width,
    halo_in, unmatched_in, owner_in, cand_in, lengths_in, choice_in, desc,
    phantom, best,
    halo, unmatched, owner, cand, lengths, choice,
    send, recv, send_meta, recv_meta, mine_table, table, scores, bias, taken,
    back, recv_back, back_best, recv_best,
    row_ss, row_rs, meta_ss, meta_rs, back_ss, back_rs, best_ss, best_rs, table_sem, local_sem, load_sem,
):
    me, core = lax.axis_index("space"), lax.axis_index("rep")
    snaps, halos, half = halo.shape
    k_count = cand.shape[1]
    cands = desc.shape[1]
    own = snaps // 2
    total = n * slots
    hs = slots // 2

    def core_of(x):
        return lax.rem(core + x, 2)

    def remote(src, dst, ss, rs, peer, x):
        return pltpu.make_async_remote_copy(
            src_ref=src, dst_ref=dst, send_sem=ss, recv_sem=rs,
            device_id=(peer, core_of(x)), device_id_type=MESH,
        )

    def each_chip(f):
        @pl.loop(1, n)
        def _(d):
            f(lax.rem(me + d, n))

    def each_peer(f):
        def both(peer):
            f(peer, 0)
            f(peer, 1)

        each_chip(both)
        f(me, 1)

    barrier = pltpu.get_barrier_semaphore()
    each_peer(
        lambda peer, x: pl.semaphore_signal(
            barrier, inc=1, device_id=(peer, core_of(x)), device_id_type=MESH
        ),
    )
    own_table = pltpu.make_async_copy(desc.at[pl.ds(own * core, own)], mine_table, local_sem.at[0])
    own_table.start()
    loads = [
        pltpu.make_async_copy(src, dst, load_sem.at[i])
        for i, (src, dst) in enumerate(
            [
                (owner_in, owner), (unmatched_in, unmatched), (cand_in, cand),
                (lengths_in, lengths), (choice_in, choice), (halo_in, halo),
            ]
        )
    ]
    for load in loads:
        load.start()
    for load in loads:
        load.wait()

    upper = hot(iota((halos, halos), 0) < iota((halos, halos), 1))
    route = []
    for x in range(2):
        for ls in range(own):
            s = own * core_of(x) + ls
            dest = owner[s]
            named = iota((n, halos), 0) == dest
            onehot = hot(named)
            rank = jnp.sum(jnp.where(named, dot(onehot, upper), 0.0), axis=0, keepdims=True)
            rank = rank.astype(jnp.int32)
            live = unmatched[pl.ds(s, 1), :] == 1
            target = jnp.where(live, dest * slots + rank, -1)
            route.append((onehot, rank, target, live))

    meta = None
    for ls in range(own):
        s = own * core + ls
        _, rank, _, live = route[ls]
        listed = code(cand[s], cands)
        k_ids = iota((k_count, halos), 0)
        pick = jnp.sum(jnp.where(k_ids == choice[pl.ds(s, 1), :], listed, 0), axis=0, keepdims=True)
        listed = jnp.where(k_ids < lengths[pl.ds(s, 1), :], listed, 0)
        block = jnp.concatenate(
            [listed, jnp.broadcast_to(pick, (GROUP - k_count, halos))], axis=0
        ).astype(F32)
        for g in range(2):
            lead = (g * own + ls) * GROUP
            parts = [jnp.zeros((lead, halos), F32)] if lead else []
            parts.append(block)
            if lead + GROUP < 128:
                parts.append(jnp.zeros((128 - lead - GROUP, halos), F32))
            here = live & (rank >= g * hs) & (rank < (g + 1) * hs)
            row = jnp.where(here, owner[s] * hs + rank - g * hs, -1)
            term = lax.dot_general(
                hot(iota((n * hs, halos), 0) == row),
                (jnp.concatenate(parts, axis=0) if len(parts) > 1 else block).astype(BF16),
                NT, preferred_element_type=F32,
            )
            meta = term if meta is None else meta + term
    send_meta[...] = meta.astype(BF16).reshape(n, hs, 128)

    for ls in range(own):
        for x in range(2):
            place = hot(iota((total, halos), 0) == route[x * own + ls][2])
            rows = dot(place, halo[own * core_of(x) + ls]).astype(BF16)
            send[ls, x] = rows.reshape(n, slots, half)

    pl.semaphore_wait(barrier, 2 * n - 1)

    def row_copy(ls, peer, x, at):
        return remote(
            send.at[ls, x, peer], recv.at[ls, x, at], row_ss.at[ls, x, peer], row_rs.at[ls, x, at], peer, x
        )

    def meta_copy(peer, at):
        return remote(send_meta.at[peer], recv_meta.at[at], meta_ss.at[peer], meta_rs.at[at], peer, 0)

    table_copy = remote(
        desc.at[pl.ds(own * core_of(1), own)], table, table_sem.at[0], table_sem.at[1], me, 1
    )
    table_copy.start()
    each_chip(lambda peer: meta_copy(peer, me).start())
    for ls in range(own):
        each_peer(lambda peer, x: row_copy(ls, peer, x, me).start())
    local_meta = pltpu.make_async_copy(send_meta.at[me], recv_meta.at[me], local_sem.at[1])
    local_meta.start()
    local_rows = []
    for ls in range(own):
        local_rows.append(
            pltpu.make_async_copy(send.at[ls, 0, me], recv.at[ls, 0, me], local_sem.at[2 + ls])
        )
        local_rows[-1].start()

    step = 64
    entry = iota((n * hs, total), 0)
    column = iota((n * hs, total), 1)
    inside = column % slots
    unpack = [
        hot((entry == (column // slots) * hs + inside - g * hs) & (inside // hs == g)) for g in range(2)
    ]
    local_meta.wait()
    each_chip(lambda peer: meta_copy(peer, peer).wait_recv())
    arrived = recv_meta[...].reshape(n * hs, 128).astype(F32).T.astype(BF16)
    picks = []
    for ls in range(own):
        lists = sum(
            dot(arrived[(g * own + ls) * GROUP : (g * own + ls + 1) * GROUP], unpack[g]) for g in range(2)
        )
        picks.append(lists[k_count : k_count + 1])

        @pl.loop(0, cands // step)
        def _(i):
            ids = code(iota((step, total), 0) + i * step, cands).astype(F32)
            mask = ids == lists[0:1]
            for k in range(1, k_count):
                mask = mask | (ids == lists[k : k + 1])
            bias[ls, pl.ds(pl.multiple_of(i * step, step), step), :] = jnp.where(mask, 0.0, NEG)

    own_table.wait()
    table_copy.wait_recv()
    for ls in range(own):
        chosen = jnp.broadcast_to(picks[ls], (128, total)).T[:, 0:1]
        select = hot(chosen == code(iota((total, cands), 1), cands).astype(F32))
        taken[ls, 0] = dot(select, mine_table[ls])
        taken[ls, 1] = dot(select, table[ls])

    def back_copy(ls, peer, x, at):
        return remote(
            back.at[ls, x, peer], recv_back.at[ls, x, at],
            back_ss.at[ls, x, peer], back_rs.at[ls, x, at], peer, x,
        )

    def best_copy(peer, x, at):
        return remote(back_best.at[peer], recv_best.at[x, at], best_ss.at[x, peer], best_rs.at[x, at], peer, x)

    scale = 1.0 / math.sqrt(width)
    lane = iota((total, 128), 0)
    fold = None
    local_backs = []
    for ls in range(own):
        local_rows[ls].wait()
        each_peer(lambda peer, x: row_copy(ls, peer, x, peer).wait_recv())
        halves = [recv[ls, x].reshape(total, half) for x in range(2)]
        scores[...] = lax.dot_general(
            jnp.concatenate([mine_table[ls], table[ls]], axis=1), jnp.concatenate(halves, axis=1), NT,
            preferred_element_type=F32,
        )

        def chunk(i, carry):
            top, picked, claimed = carry
            at = pl.ds(pl.multiple_of(i * step, step), step)
            value = scores[at, :]
            masked = value + bias[ls, at, :]
            claim = jnp.max(masked, axis=1, keepdims=True)
            chosen = code(iota((step, total), 0) + i * step, cands).astype(F32) == picks[ls]

            def least(v):
                return jnp.max(v.reshape(step // 8, 8, total), axis=0)

            return (
                jnp.maximum(top, least(masked)),
                jnp.maximum(picked, least(jnp.where(chosen, value, NEG))),
                jnp.maximum(claimed, least(jnp.where(chosen, claim, NEG))),
            )

        start = jnp.full((8, total), NEG, F32)
        top, picked, claimed = [
            jnp.max(v, axis=0, keepdims=True)
            for v in lax.fori_loop(0, cands // step, chunk, (start, start, start))
        ]

        def quality(v):
            v = v * scale
            return 1.0 + jnp.maximum(v, 0.0) + jnp.log(1.0 + jnp.exp(-jnp.abs(v)))

        mine = quality(picked)
        share = mine / (mine + quality(claimed))
        share = jnp.broadcast_to(share, (128, total)).T
        for x in range(2):
            blend = (1.0 - share) * halves[x].astype(F32) + share * taken[ls, x]
            back[ls, x] = blend.astype(BF16).reshape(n, slots, half)

        top = jnp.where(top > NEG * 0.5, top * scale, 0.0)
        spread = jnp.where(
            iota((n, total), 0) == iota((n, total), 1) // slots, jnp.broadcast_to(top, (n, total)), 0.0
        ).astype(BF16)
        term = dot(spread, hot(iota((total, 128), 1) == ls * slots + lane % slots))
        fold = term if fold is None else fold + term
        if ls == own - 1:
            back_best[...] = fold.reshape(n, 1, 128)
            each_peer(lambda peer, x: best_copy(peer, x, me).start())
        each_peer(lambda peer, x: back_copy(ls, peer, x, me).start())
        local_backs.append(
            pltpu.make_async_copy(back.at[ls, 0, me], recv_back.at[ls, 0, me], local_sem.at[2 + own + ls])
        )
        local_backs[-1].start()
    local_best = pltpu.make_async_copy(back_best.at[me], recv_best.at[0, me], local_sem.at[2 + 2 * own])
    local_best.start()

    columns = [
        jnp.broadcast_to(target.astype(F32), (128, halos)).T[:, 0:1] for _, _, target, _ in route
    ]
    for ls in range(own):
        local_backs[ls].wait()
        each_peer(lambda peer, x: back_copy(ls, peer, x, peer).wait_recv())
        for x in range(2):
            s = own * core_of(x) + ls
            column = columns[x * own + ls]
            place = hot(iota((halos, total), 1).astype(F32) == column)
            rows = dot(place, recv_back[ls, x].reshape(total, half))
            phantom[s] = jnp.where(column < 0.0, halo[s].astype(F32), rows).astype(BF16)

    local_best.wait()
    each_peer(lambda peer, x: best_copy(peer, x, peer).wait_recv())
    tops = []
    for x in range(2):
        brought = recv_best[x].reshape(n, 128).astype(BF16)
        for ls in range(own):
            onehot, rank, _, live = route[x * own + ls]
            spread = lax.dot_general(brought, onehot, TN, preferred_element_type=F32)
            here = jnp.where(iota((128, halos), 0) == ls * slots + rank, spread, 0.0)
            tops.append(jnp.where(live, jnp.sum(here, axis=0, keepdims=True), 0.0))
    first, second = jnp.concatenate(tops[:own], axis=0), jnp.concatenate(tops[own:], axis=0)
    even = core == 0
    best[...] = jnp.concatenate(
        [jnp.where(even, first, second), jnp.where(even, second, first)], axis=0
    ).astype(BF16)

    table_copy.wait_send()
    each_chip(lambda peer: meta_copy(peer, me).wait_send())
    for ls in range(own):
        each_peer(lambda peer, x: row_copy(ls, peer, x, me).wait_send())
        each_peer(lambda peer, x: back_copy(ls, peer, x, me).wait_send())
    each_peer(lambda peer, x: best_copy(peer, x, me).wait_send())


def hand_over(phantom_in, best_in, phantom, best):
    phantom[...] = phantom_in[...]
    best[...] = best_in[...]


def body(n, halo_rows, unmatched, owner_id, cand_index, lengths, choice_index, desc_rows):
    snaps, halos, half = halo_rows.shape
    cands = desc_rows.shape[1]
    own = snaps // 2
    slots = max(2 * halos // n, 16)
    total = n * slots
    dma = pltpu.SemaphoreType.DMA
    results = pl.pallas_call(
        functools.partial(kernel, n, slots, 2 * half),
        out_shape=(
            pltpu.VMEM((snaps, halos, half), BF16),
            pltpu.VMEM((snaps, halos), BF16),
        ),
        in_specs=[pl.BlockSpec(memory_space=pl.ANY)] * 7,
        out_specs=(pl.BlockSpec(memory_space=pltpu.VMEM),) * 2,
        scratch_shapes=[
            pltpu.VMEM(halo_rows.shape, BF16),
            pltpu.VMEM(unmatched.shape, jnp.int32),
            pltpu.VMEM((snaps, 1, halos), jnp.int32),
            pltpu.VMEM((snaps, cand_index.shape[2], halos), jnp.int32),
            pltpu.VMEM(lengths.shape, jnp.int32),
            pltpu.VMEM(choice_index.shape, jnp.int32),
            pltpu.VMEM((own, 2, n, slots, half), BF16),
            pltpu.VMEM((own, 2, n, slots, half), BF16),
            pltpu.VMEM((n, slots // 2, 128), BF16),
            pltpu.VMEM((n, slots // 2, 128), BF16),
            pltpu.VMEM((own, cands, half), BF16),
            pltpu.VMEM((own, cands, half), BF16),
            pltpu.VMEM((cands, total), F32),
            pltpu.VMEM((own, cands, total), F32),
            pltpu.VMEM((own, 2, total, half), F32),
            pltpu.VMEM((own, 2, n, slots, half), BF16),
            pltpu.VMEM((own, 2, n, slots, half), BF16),
            pltpu.VMEM((n, 1, 128), F32),
            pltpu.VMEM((2, n, 1, 128), F32),
            dma((own, 2, n)), dma((own, 2, n)), dma((n,)), dma((n,)),
            dma((own, 2, n)), dma((own, 2, n)), dma((2, n)), dma((2, n)),
            dma((2,)), dma((3 + 2 * own,)), dma((6,)),
        ],
        compiler_params=pltpu.CompilerParams(collective_id=0, has_side_effects=True),
    )(
        halo_rows,
        unmatched,
        jnp.swapaxes(owner_id, 1, 2),
        jnp.swapaxes(cand_index, 1, 2),
        lengths,
        choice_index,
        desc_rows,
    )
    shapes = tuple(jax.ShapeDtypeStruct(v.shape, v.dtype) for v in results)
    return pl.pallas_call(
        hand_over,
        out_shape=shapes,
        in_specs=[pl.BlockSpec(memory_space=pltpu.VMEM)] * 2,
        out_specs=(pl.BlockSpec(memory_space=pltpu.VMEM),) * 2,
    )(*[pltpu.with_memory_space_constraint(v, pltpu.VMEM) for v in results])


def solution(mesh):
    in_specs = (
        P(None, "space", "rep"),
        P(None, "space"),
        P(None, "space", None),
        P(None, "space", None),
        P(None, "space"),
        P(None, "space"),
        P(None, "space", "rep"),
    )
    out_specs = (P(None, "space", "rep"), P(None, "space"))
    return jax.shard_map(
        functools.partial(body, mesh.shape["space"]),
        mesh=mesh, in_specs=in_specs, out_specs=out_specs, check_vma=False,
    )
```

profile of v0, /device:TPU:0, one launch (start us, length us, event | category | flops | bytes accessed | tf_op | source)
XLA Modules:
  0.0 30.4 jit_solution(16636826928156589065)
XLA Ops:
  0.6 29.0 %shard_map.86 = (bf16[4,128,128]{2,1,0:T(8,128)(2,1)S(1)}, bf16[4,128]{1,0:T(4,128)(2,1)S(1)}) custom-call(bf16[4,128,128]{2,1,0:T(8,128)(2,1)} %halo_in.1, s32[4,128]{1,0:T(4,128)} %unmatched_in.1, s32[4,1,128]{2,1,0:T(1,128)} %bitcast.3, s32[4,16,128]{2,1,0:T(8,128)} %bitcast.2, s32[4,128]{1,0:T(4,128)} %lengths_in.1, s32[4,128]{1,0:T(4,128)} %choice_in.1, ...), custom_call_target="tpu_custom_call" | custom-call | tf_op jit(solution)/shard_map/pallas_call | solution.py:325
  29.7 0.7 %shard_map.87 = (bf16[4,128,128]{2,1,0:T(8,128)(2,1)}, bf16[4,128]{1,0:T(4,128)(2,1)}) custom-call(bf16[4,128,128]{2,1,0:T(8,128)(2,1)S(1)} %get-tuple-element.4.phantom_in, bf16[4,128]{1,0:T(4,128)(2,1)S(1)} %get-tuple-element.5.best_in), custom_call_target="tpu_custom_call" | custom-call | tf_op jit(solution)/shard_map/pallas_call | solution.py:368
where the time goes:
time: 30.5 us; the launch traced here: 30.4 us
  Pallas kernels  29.7 us (97%)
  between operations  0.64 us (2%)
    pallas_call x1, Pallas kernels, body(): pl.pallas_call(functools.partial(kernel, n, slots, 2 * half), out_shape=(...  29 us
    pallas_call x1, Pallas kernels, body(): pl.pallas_call(hand_over, out_shape=shapes, in_specs=[pl.BlockSpec(memory...  0.67 us

commit v1 on v0

v1 whole, which is shorter than its diff:
```python
import functools
import math

import jax
import jax.numpy as jnp
from jax import lax
from jax.experimental import pallas as pl
from jax.experimental.pallas import tpu as pltpu
from jax.sharding import PartitionSpec as P

MESH = pl.DeviceIdType.MESH
F32 = jnp.float32
BF16 = jnp.bfloat16
NEG = -1e30
GROUP = 32
NT = (((1,), (1,)), ((), ()))


def iota(shape, dim):
    return lax.broadcasted_iota(jnp.int32, shape, dim)


def dot(a, b):
    return jnp.dot(a, b, preferred_element_type=F32)


def dot_nt(a, b):
    return lax.dot_general(a, b, NT, preferred_element_type=F32)


def hot(mask):
    return jnp.where(mask, 1.0, 0.0).astype(BF16)


def code(index, cands):
    return index - cands // 2 + jnp.where(index >= cands // 2, 1, 0)


def kernel(
    n, slots, width,
    halo_in, unmatched_in, owner_in, cand_in, lengths_in, choice_in, desc_in,
    phantom, best,
    halo, unmatched, owner, cand, lengths, choice, desc, table,
    send, recv, send_meta, recv_meta, scores, bias, pick, recv_pick, res, recv_res,
    row_sem, meta_sem, pick_ss, pick_rs, res_ss, res_rs, table_sem, load_sem,
):
    me, core = lax.axis_index("space"), lax.axis_index("rep")
    snaps, halos, half = halo.shape
    k_count = cand.shape[1]
    cands = desc.shape[1]
    own = snaps // 2
    total = n * slots
    hs = slots // 2

    def core_of(x):
        return lax.rem(core + x, 2)

    def remote(src, dst, ss, rs, peer, x):
        return pltpu.make_async_remote_copy(
            src_ref=src, dst_ref=dst, send_sem=ss, recv_sem=rs,
            device_id=(peer, core_of(x)), device_id_type=MESH,
        )

    def whole(ref, ss, rs):
        return remote(ref, ref, ss, rs, me, 1)

    def each_chip(f):
        @pl.loop(1, n)
        def _(d):
            f(lax.rem(me + d, n))

    def each_peer(f):
        def both(peer):
            f(peer, 0)
            f(peer, 1)

        each_chip(both)
        f(me, 1)

    barrier = pltpu.get_barrier_semaphore()
    each_peer(
        lambda peer, x: pl.semaphore_signal(
            barrier, inc=1, device_id=(peer, core_of(x)), device_id_type=MESH
        ),
    )
    loads = [
        pltpu.make_async_copy(src, dst, load_sem.at[i])
        for i, (src, dst) in enumerate(
            [
                (owner_in, owner), (unmatched_in, unmatched), (cand_in, cand),
                (lengths_in, lengths), (choice_in, choice), (halo_in, halo), (desc_in, desc),
            ]
        )
    ]
    for load in loads:
        load.start()
    for load in loads[:5]:
        load.wait()

    order = [(x, ls) for x in range(2) for ls in range(own)]
    named = [iota((n, halos), 0) == owner[own * core_of(x) + ls] for x, ls in order]
    onehot = hot(jnp.concatenate(named, axis=0))
    before = dot(onehot, hot(iota((halos, halos), 0) < iota((halos, halos), 1)))
    route = []
    for i, (x, ls) in enumerate(order):
        s = own * core_of(x) + ls
        rank = jnp.sum(
            jnp.where(named[i], before[i * n : (i + 1) * n], 0.0), axis=0, keepdims=True
        ).astype(jnp.int32)
        live = unmatched[pl.ds(s, 1), :] == 1
        dest = owner[s]
        route.append((dest, rank, jnp.where(live, dest * slots + rank, -1), live))

    blocks, rows = [], []
    for i, (x, ls) in enumerate(order):
        s = own * core_of(x) + ls
        dest, rank, _, live = route[i]
        listed = code(cand[s], cands)
        k_ids = iota((k_count, halos), 0)
        taken = jnp.sum(jnp.where(k_ids == choice[pl.ds(s, 1), :], listed, 0), axis=0, keepdims=True)
        taken = jnp.broadcast_to(taken, (8, halos))
        none = jnp.zeros((8, halos), jnp.int32)
        if x == 0:
            listed = jnp.where(k_ids < lengths[pl.ds(s, 1), :], listed, 0)
            parts = [listed, taken, none]
        else:
            parts = [jnp.zeros((k_count, halos), jnp.int32), none, taken]
        parts = [jnp.zeros((GROUP * ls, halos), jnp.int32)] * (ls > 0) + parts
        if ls < own - 1:
            parts.append(jnp.zeros((GROUP * (own - 1 - ls), halos), jnp.int32))
        blocks.append(jnp.concatenate(parts, axis=0).astype(F32).astype(BF16))
        rows.append(
            [
                jnp.where(live & (rank >= g * hs) & (rank < (g + 1) * hs), dest * hs + rank - g * hs, -1)
                for g in range(2)
            ]
        )
    block = jnp.concatenate(blocks, axis=1)
    blank = jnp.zeros_like(block)
    meta = sum(
        dot_nt(
            jnp.concatenate([hot(iota((n * hs, halos), 0) == r[g]) for r in rows], axis=1),
            jnp.concatenate([blank, block] if g else [block, blank], axis=0),
        )
        for g in range(2)
    )
    send_meta[...] = meta.astype(BF16).reshape(n, hs, 128)

    loads[5].wait()
    for i, (x, ls) in enumerate(order):
        place = hot(iota((total, halos), 0) == route[i][2])
        packed = dot(place, halo[own * core_of(x) + ls]).astype(BF16)
        send[x * n : (x + 1) * n, ls] = packed.reshape(n, slots, half)

    pl.semaphore_wait(barrier, 2 * n - 1)

    each_chip(
        lambda peer: remote(
            send_meta.at[peer], recv_meta.at[me], meta_sem.at[0], meta_sem.at[1], peer, 0
        ).start()
    )
    each_peer(
        lambda peer, x: remote(
            send.at[x * n + peer], recv.at[x * n + me], row_sem.at[0], row_sem.at[1], peer, x
        ).start()
    )
    table_copy = remote(
        desc_in.at[pl.ds(own * core_of(1), own)], table, table_sem.at[0], table_sem.at[1], me, 1
    )
    table_copy.start()
    recv_meta[me] = send_meta[me]
    recv[me] = send[me]

    lines = [v.astype(F32) for dest, rank, target, live in route for v in (dest, jnp.where(live, rank, -halos), target)]
    lines = jnp.concatenate(lines + [jnp.zeros((128 - len(lines), halos), F32)], axis=0).T
    back = []
    lane = iota((halos, 128), 1).astype(F32)
    for i in range(snaps):
        dest, rank, target = [lines[:, 3 * i + j : 3 * i + j + 1] for j in range(3)]
        back.append(
            (
                hot(iota((halos, n), 1).astype(F32) == dest),
                (lane == rank) | (lane == rank + slots),
                lane == rank + 2 * slots,
                hot(iota((halos, total), 1).astype(F32) == target),
            )
        )
    entry = iota((n * hs, total), 0)
    column = iota((n * hs, total), 1)
    inside = column % slots
    unpack = [
        hot((entry == (column // slots) * hs + inside - g * hs) & (inside // hs == g)) for g in range(2)
    ]
    loads[6].wait()

    whole(recv_meta.at[pl.ds(0, n - 1)], meta_sem.at[0], meta_sem.at[1]).wait_recv()
    arrived = recv_meta[...].reshape(n * hs, 128).astype(F32)
    ids = code(iota((n * hs, cands), 1), cands).astype(F32)
    for ls in range(own):
        for x in range(2):
            lanes = [(g * own + ls) * GROUP + k_count + 8 * x for g in range(2)]
            select = jnp.concatenate([hot(arrived[:, at : at + 1] == ids) for at in lanes], axis=0)
            chosen = dot(select, desc[own * core_of(x) + ls]).astype(BF16)
            for g in range(2):
                pick[ls, :, x, g * hs : (g + 1) * hs, :] = chosen[
                    g * n * hs : (g + 1) * n * hs
                ].reshape(n, hs, half)
        each_chip(
            lambda peer: remote(
                pick.at[ls, peer], recv_pick.at[ls, me], pick_ss.at[ls], pick_rs.at[ls], peer, 0
            ).start()
        )
        recv_pick[ls, me] = pick[ls, me]

    step = 64
    arrived = arrived.T.astype(BF16)
    picks = []
    for ls in range(own):
        lists = sum(
            dot(arrived[(g * own + ls) * GROUP : (g * own + ls + 1) * GROUP], unpack[g]) for g in range(2)
        )
        picks.append(lists[k_count : k_count + 1])

        @pl.loop(0, cands // step)
        def _(i):
            ids = code(iota((step, total), 0) + i * step, cands).astype(F32)
            mask = ids == lists[0:1]
            for k in range(1, k_count):
                mask = mask | (ids == lists[k : k + 1])
            bias[ls, pl.ds(pl.multiple_of(i * step, step), step), :] = jnp.where(mask, 0.0, NEG)

    scale = 1.0 / math.sqrt(width)
    owned = iota((n, total), 0) == iota((n, total), 1) // slots
    fold = jnp.concatenate(
        [hot(iota((total, 128), 1) == part * slots + iota((total, 128), 0) % slots) for part in range(3)],
        axis=0,
    )

    table_copy.wait_recv()
    whole(recv.at[pl.ds(0, 2 * n - 1)], row_sem.at[0], row_sem.at[1]).wait_recv()
    for ls in range(own):
        scores[...] = dot_nt(
            jnp.concatenate([desc[own * core + ls], table[ls]], axis=1),
            jnp.concatenate(
                [recv[x * n : (x + 1) * n, ls].reshape(total, half) for x in range(2)], axis=1
            ),
        )

        def chunk(i, carry):
            top, picked, claimed = carry
            at = pl.ds(pl.multiple_of(i * step, step), step)
            value = scores[at, :]
            masked = value + bias[ls, at, :]
            claim = jnp.max(masked, axis=1, keepdims=True)
            chosen = code(iota((step, total), 0) + i * step, cands).astype(F32) == picks[ls]

            def least(v):
                return jnp.max(v.reshape(step // 8, 8, total), axis=0)

            return (
                jnp.maximum(top, least(masked)),
                jnp.maximum(picked, least(jnp.where(chosen, value, NEG))),
                jnp.maximum(claimed, least(jnp.where(chosen, claim, NEG))),
            )

        start = jnp.full((8, total), NEG, F32)
        top, picked, claimed = [
            jnp.max(v, axis=0, keepdims=True)
            for v in lax.fori_loop(0, cands // step, chunk, (start, start, start))
        ]

        def quality(v):
            v = v * scale
            return 1.0 + jnp.maximum(v, 0.0) + jnp.log(1.0 + jnp.exp(-jnp.abs(v)))

        mine = quality(picked)
        share = mine / (mine + quality(claimed))
        high = share.astype(BF16).astype(F32)
        top = jnp.where(top > NEG * 0.5, top * scale, 0.0)
        spread = jnp.concatenate(
            [jnp.where(owned, jnp.broadcast_to(v, (n, total)), 0.0) for v in (high, share - high, top)],
            axis=1,
        ).astype(BF16)
        res[ls] = dot(spread, fold).reshape(n, 1, 128)
        each_peer(
            lambda peer, x: remote(
                res.at[ls, peer], recv_res.at[ls, x * n + me], res_ss.at[ls], res_rs.at[ls], peer, x
            ).start()
        )
        recv_res[ls, me] = res[ls, me]

    ones = jnp.ones((128, half), BF16)
    tops = []
    for ls in range(own):
        whole(recv_pick.at[ls, pl.ds(0, n - 1)], pick_ss.at[ls], pick_rs.at[ls]).wait_recv()
        rows = [
            dot(back[x * own + ls][3], recv_pick[ls, :, x].reshape(total, half)) for x in range(2)
        ]
        whole(recv_res.at[ls, pl.ds(0, 2 * n - 1)], res_ss.at[ls], res_rs.at[ls]).wait_recv()
        for x in range(2):
            s = own * core_of(x) + ls
            named, shared, topped, _ = back[x * own + ls]
            brought = recv_res[ls, x * n : (x + 1) * n].reshape(n, 128).astype(BF16)
            spread = dot(named, brought)
            share = dot(jnp.where(shared, spread, 0.0).astype(BF16), ones)
            phantom[s] = ((1.0 - share) * halo[s].astype(F32) + share * rows[x]).astype(BF16)
            tops.append(dot_nt(ones[0:8], jnp.where(topped, spread, 0.0).astype(BF16))[0:1])
    first, second = jnp.concatenate(tops[0::2], axis=0), jnp.concatenate(tops[1::2], axis=0)
    even = core == 0
    best[...] = jnp.concatenate(
        [jnp.where(even, first, second), jnp.where(even, second, first)], axis=0
    ).astype(BF16)

    table_copy.wait_send()
    whole(send_meta.at[pl.ds(0, n - 1)], meta_sem.at[0], meta_sem.at[1]).wait_send()
    whole(send.at[pl.ds(0, 2 * n - 1)], row_sem.at[0], row_sem.at[1]).wait_send()
    for ls in range(own):
        whole(pick.at[ls, pl.ds(0, n - 1)], pick_ss.at[ls], pick_rs.at[ls]).wait_send()
        whole(recv_res.at[ls, pl.ds(0, 2 * n - 1)], res_ss.at[ls], res_rs.at[ls]).wait_send()


def hand_over(phantom_in, best_in, phantom, best):
    phantom[...] = phantom_in[...]
    best[...] = best_in[...]


def body(n, halo_rows, unmatched, owner_id, cand_index, lengths, choice_index, desc_rows):
    snaps, halos, half = halo_rows.shape
    cands = desc_rows.shape[1]
    own = snaps // 2
    slots = max(2 * halos // n, 16)
    total = n * slots
    dma = pltpu.SemaphoreType.DMA
    results = pl.pallas_call(
        functools.partial(kernel, n, slots, 2 * half),
        out_shape=(
            pltpu.VMEM((snaps, halos, half), BF16),
            pltpu.VMEM((snaps, halos), BF16),
        ),
        in_specs=[pl.BlockSpec(memory_space=pl.ANY)] * 7,
        out_specs=(pl.BlockSpec(memory_space=pltpu.VMEM),) * 2,
        scratch_shapes=[
            pltpu.VMEM(halo_rows.shape, BF16),
            pltpu.VMEM(unmatched.shape, jnp.int32),
            pltpu.VMEM((snaps, 1, halos), jnp.int32),
            pltpu.VMEM((snaps, cand_index.shape[2], halos), jnp.int32),
            pltpu.VMEM(lengths.shape, jnp.int32),
            pltpu.VMEM(choice_index.shape, jnp.int32),
            pltpu.VMEM((snaps, cands, half), BF16),
            pltpu.VMEM((own, cands, half), BF16),
            pltpu.VMEM((2 * n, own, slots, half), BF16),
            pltpu.VMEM((2 * n, own, slots, half), BF16),
            pltpu.VMEM((n, slots // 2, 128), BF16),
            pltpu.VMEM((n, slots // 2, 128), BF16),
            pltpu.VMEM((cands, total), F32),
            pltpu.VMEM((own, cands, total), F32),
            pltpu.VMEM((own, n, 2, slots, half), BF16),
            pltpu.VMEM((own, n, 2, slots, half), BF16),
            pltpu.VMEM((own, n, 1, 128), F32),
            pltpu.VMEM((own, 2 * n, 1, 128), F32),
            dma((2,)), dma((2,)), dma((own,)), dma((own,)), dma((own,)), dma((own,)), dma((2,)), dma((7,)),
        ],
        compiler_params=pltpu.CompilerParams(collective_id=0, has_side_effects=True),
    )(
        halo_rows,
        unmatched,
        jnp.swapaxes(owner_id, 1, 2),
        jnp.swapaxes(cand_index, 1, 2),
        lengths,
        choice_index,
        desc_rows,
    )
    shapes = tuple(jax.ShapeDtypeStruct(v.shape, v.dtype) for v in results)
    return pl.pallas_call(
        hand_over,
        out_shape=shapes,
        in_specs=[pl.BlockSpec(memory_space=pltpu.VMEM)] * 2,
        out_specs=(pl.BlockSpec(memory_space=pltpu.VMEM),) * 2,
    )(*[pltpu.with_memory_space_constraint(v, pltpu.VMEM) for v in results])


def solution(mesh):
    in_specs = (
        P(None, "space", "rep"),
        P(None, "space"),
        P(None, "space", None),
        P(None, "space", None),
        P(None, "space"),
        P(None, "space"),
        P(None, "space", "rep"),
    )
    out_specs = (P(None, "space", "rep"), P(None, "space"))
    return jax.shard_map(
        functools.partial(body, mesh.shape["space"]),
        mesh=mesh, in_specs=in_specs, out_specs=out_specs, check_vma=False,
    )
```

time: 30.5 us -> 27.6 us (0.905)
  Pallas kernels: 29.7 us -> 26.7 us
    pallas_call x1, Pallas kernels: 29 us -> 26.1 us  [body(): pl.pallas_call(functools.partial(kernel, n, slots, 2 * half), out_shape=(...]
where the time goes in v1:
time: 27.6 us; the launch traced here: 27.4 us
  Pallas kernels  26.7 us (97%)
  between operations  0.64 us (2%)
    pallas_call x1, Pallas kernels, body(): pl.pallas_call(functools.partial(kernel, n, slots, 2 * half), out_shape=(...  26.1 us
    pallas_call x1, Pallas kernels, body(): pl.pallas_call(hand_over, out_shape=shapes, in_specs=[pl.BlockSpec(memory...  0.67 us

profile of v1, /device:TPU:0, one launch (start us, length us, event | category | flops | bytes accessed | tf_op | source)
XLA Modules:
  0.0 27.4 jit_solution(2407766746973887102)
XLA Ops:
  0.6 26.1 %shard_map.86 = (bf16[4,128,128]{2,1,0:T(8,128)(2,1)S(1)}, bf16[4,128]{1,0:T(4,128)(2,1)S(1)}) custom-call(bf16[4,128,128]{2,1,0:T(8,128)(2,1)} %halo_in.1, s32[4,128]{1,0:T(4,128)} %unmatched_in.1, s32[4,1,128]{2,1,0:T(1,128)} %bitcast.3, s32[4,16,128]{2,1,0:T(8,128)} %bitcast.2, s32[4,128]{1,0:T(4,128)} %lengths_in.1, s32[4,128]{1,0:T(4,128)} %choice_in.1, ...), custom_call_target="tpu_custom_call" | custom-call | tf_op jit(solution)/shard_map/pallas_call | solution.py:334
  26.7 0.7 %shard_map.87 = (bf16[4,128,128]{2,1,0:T(8,128)(2,1)}, bf16[4,128]{1,0:T(4,128)(2,1)}) custom-call(bf16[4,128,128]{2,1,0:T(8,128)(2,1)S(1)} %get-tuple-element.4.phantom_in, bf16[4,128]{1,0:T(4,128)(2,1)S(1)} %get-tuple-element.5.best_in), custom_call_target="tpu_custom_call" | custom-call | tf_op jit(solution)/shard_map/pallas_call | solution.py:374

commit v2 on v1

--- a/solution.py
+++ b/solution.py
@@ -41,8 +41,8 @@
     halo_in, unmatched_in, owner_in, cand_in, lengths_in, choice_in, desc_in,
     phantom, best,
     halo, unmatched, owner, cand, lengths, choice, desc, table,
-    send, recv, send_meta, recv_meta, scores, bias, pick, recv_pick, res, recv_res,
-    row_sem, meta_sem, pick_ss, pick_rs, res_ss, res_rs, table_sem, load_sem,
+    send, recv, send_want, recv_want, send_meta, recv_meta, scores, bias, pick, recv_pick, res, recv_res,
+    row_sem, want_sem, meta_sem, pick_sem, res_sem, table_sem, load_sem,
 ):
     me, core = lax.axis_index("space"), lax.axis_index("rep")
     snaps, halos, half = halo.shape
@@ -53,7 +53,7 @@
     hs = slots // 2
 
     def core_of(x):
-        return lax.rem(core + x, 2)
+        return 1 - core if x else core
 
     def remote(src, dst, ss, rs, peer, x):
         return pltpu.make_async_remote_copy(
@@ -65,9 +65,21 @@
         return remote(ref, ref, ss, rs, me, 1)
 
     def each_chip(f):
-        @pl.loop(1, n)
-        def _(d):
-            f(lax.rem(me + d, n))
+        if n % 4 or n > 32:
+
+            @pl.loop(1, n)
+            def _(d):
+                peer = me + d
+                f(jnp.where(peer >= n, peer - n, peer))
+
+            return
+        block, place = me // 4, lax.rem(me, 4)
+        for d in [*range(1, n // 4), 0]:
+            to = block + d
+            to = jnp.where(to >= n // 4, to - n // 4, to) * 4
+            for q in (3, 1, 2, 0):
+                if d or q:
+                    f(to + jnp.bitwise_xor(place, q))
 
     def each_peer(f):
         def both(peer):
@@ -111,20 +123,33 @@
         dest = owner[s]
         route.append((dest, rank, jnp.where(live, dest * slots + rank, -1), live))
 
-    blocks, rows = [], []
+    k_ids = iota((k_count, halos), 0)
+    wants, coded = [], []
     for i, (x, ls) in enumerate(order):
         s = own * core_of(x) + ls
-        dest, rank, _, live = route[i]
-        listed = code(cand[s], cands)
-        k_ids = iota((k_count, halos), 0)
-        taken = jnp.sum(jnp.where(k_ids == choice[pl.ds(s, 1), :], listed, 0), axis=0, keepdims=True)
-        taken = jnp.broadcast_to(taken, (8, halos))
-        none = jnp.zeros((8, halos), jnp.int32)
-        if x == 0:
-            listed = jnp.where(k_ids < lengths[pl.ds(s, 1), :], listed, 0)
-            parts = [listed, taken, none]
-        else:
-            parts = [jnp.zeros((k_count, halos), jnp.int32), none, taken]
+        _, rank, _, live = route[i]
+        coded.append(code(cand[s], cands))
+        taken = jnp.sum(
+            jnp.where(k_ids == choice[pl.ds(s, 1), :], coded[i], 0), axis=0, keepdims=True
+        )
+        wants.append(jnp.where(live & (iota((slots, halos), 0) == rank), taken, 0).astype(F32))
+    blank = jnp.zeros((slots, halos), F32)
+    table_of = [
+        jnp.concatenate([wants[i] if i == j else blank for i in range(snaps)], axis=1) for j in range(snaps)
+    ]
+    table_of.append(jnp.zeros((128 - snaps * slots, snaps * halos), F32))
+    told = dot_nt(
+        jnp.concatenate([hot(v) for v in named], axis=1), jnp.concatenate(table_of, axis=0).astype(BF16)
+    )
+    send_want[...] = told.reshape(n, 1, 128)
+
+    blocks, rows = [], []
+    for ls in range(own):
+        s = own * core + ls
+        dest, rank, _, live = route[ls]
+        listed = jnp.where(k_ids < lengths[pl.ds(s, 1), :], coded[ls], 0)
+        taken = jnp.sum(jnp.where(k_ids == choice[pl.ds(s, 1), :], coded[ls], 0), axis=0, keepdims=True)
+        parts = [listed, jnp.broadcast_to(taken, (GROUP - k_count, halos))]
         parts = [jnp.zeros((GROUP * ls, halos), jnp.int32)] * (ls > 0) + parts
         if ls < own - 1:
             parts.append(jnp.zeros((GROUP * (own - 1 - ls), halos), jnp.int32))
@@ -156,22 +181,31 @@
 
     each_chip(
         lambda peer: remote(
+            send_want.at[peer], recv_want.at[me], want_sem.at[0], want_sem.at[1], peer, 0
+        ).start()
+    )
+    each_chip(
+        lambda peer: remote(
             send_meta.at[peer], recv_meta.at[me], meta_sem.at[0], meta_sem.at[1], peer, 0
         ).start()
     )
-    each_peer(
-        lambda peer, x: remote(
-            send.at[x * n + peer], recv.at[x * n + me], row_sem.at[0], row_sem.at[1], peer, x
-        ).start()
-    )
+    def row_copy(peer, x):
+        return remote(
+            send.at[x * n + peer], recv.at[x * n + me], row_sem.at[x], row_sem.at[2 + x], peer, x
+        )
+
+    each_chip(lambda peer: row_copy(peer, 0).start())
+    each_chip(lambda peer: row_copy(peer, 1).start())
+    row_copy(me, 1).start()
     table_copy = remote(
         desc_in.at[pl.ds(own * core_of(1), own)], table, table_sem.at[0], table_sem.at[1], me, 1
     )
     table_copy.start()
+    recv_want[me] = send_want[me]
     recv_meta[me] = send_meta[me]
     recv[me] = send[me]
 
-    lines = [v.astype(F32) for dest, rank, target, live in route for v in (dest, jnp.where(live, rank, -halos), target)]
+    lines = [v.astype(F32) for dest, rank, target, live in route for v in (dest, jnp.where(live, rank, -128), target)]
     lines = jnp.concatenate(lines + [jnp.zeros((128 - len(lines), halos), F32)], axis=0).T
     back = []
     lane = iota((halos, 128), 1).astype(F32)
@@ -180,8 +214,8 @@
         back.append(
             (
                 hot(iota((halos, n), 1).astype(F32) == dest),
-                (lane == rank) | (lane == rank + slots),
-                lane == rank + 2 * slots,
+                (lane == rank + 3 * slots * (i % own)) | (lane == rank + (3 * (i % own) + 1) * slots),
+                lane == rank + (3 * (i % own) + 2) * slots,
                 hot(iota((halos, total), 1).astype(F32) == target),
             )
         )
@@ -193,27 +227,21 @@
     ]
     loads[6].wait()
 
+    ids = code(iota((total, cands), 1), cands).astype(F32)
+    from_chip = hot(iota((total, n), 1) == iota((total, n), 0) // slots)
+    its_slot = iota((total, 128), 1) % slots == iota((total, 128), 0) % slots
+    part = [hot(iota((128, 128), 0) // slots == i) for i in range(snaps)]
+
+    whole(recv_want.at[pl.ds(0, n - 1)], want_sem.at[0], want_sem.at[1]).wait_recv()
+    wanted = dot(from_chip, recv_want[...].reshape(n, 128).astype(BF16))
+    wanted = jnp.where(its_slot, wanted, 0.0).astype(BF16)
+    for i, (x, ls) in enumerate(order):
+        at = jnp.concatenate([dot(wanted, part[i])] * (cands // 128), axis=1)
+        chosen = dot(hot(at == ids), desc[own * core_of(x) + ls]).astype(BF16)
+        pick[:, 2 * ls + x] = chosen.reshape(n, slots, half)
+    step = 64
     whole(recv_meta.at[pl.ds(0, n - 1)], meta_sem.at[0], meta_sem.at[1]).wait_recv()
-    arrived = recv_meta[...].reshape(n * hs, 128).astype(F32)
-    ids = code(iota((n * hs, cands), 1), cands).astype(F32)
-    for ls in range(own):
-        for x in range(2):
-            lanes = [(g * own + ls) * GROUP + k_count + 8 * x for g in range(2)]
-            select = jnp.concatenate([hot(arrived[:, at : at + 1] == ids) for at in lanes], axis=0)
-            chosen = dot(select, desc[own * core_of(x) + ls]).astype(BF16)
-            for g in range(2):
-                pick[ls, :, x, g * hs : (g + 1) * hs, :] = chosen[
-                    g * n * hs : (g + 1) * n * hs
-                ].reshape(n, hs, half)
-        each_chip(
-            lambda peer: remote(
-                pick.at[ls, peer], recv_pick.at[ls, me], pick_ss.at[ls], pick_rs.at[ls], peer, 0
-            ).start()
-        )
-        recv_pick[ls, me] = pick[ls, me]
-
-    step = 64
-    arrived = arrived.T.astype(BF16)
+    arrived = recv_meta[...].reshape(n * hs, 128).astype(F32).T.astype(BF16)
     picks = []
     for ls in range(own):
         lists = sum(
@@ -221,25 +249,43 @@
         )
         picks.append(lists[k_count : k_count + 1])
 
-        @pl.loop(0, cands // step)
-        def _(i):
-            ids = code(iota((step, total), 0) + i * step, cands).astype(F32)
-            mask = ids == lists[0:1]
-            for k in range(1, k_count):
-                mask = mask | (ids == lists[k : k + 1])
-            bias[ls, pl.ds(pl.multiple_of(i * step, step), step), :] = jnp.where(mask, 0.0, NEG)
+        listed = lists[:k_count].astype(jnp.int32)
+        at = listed + cands // 2 - jnp.where(listed > 0, 1, 0)
+        flag = jnp.where(listed == 0, 0, jnp.left_shift(1, at & 31))
+        at = at >> 5
+        words = jnp.zeros((cands // 32, total), jnp.int32)
+        for k in range(k_count):
+            words = words | jnp.where(iota((cands // 32, total), 0) == at[k : k + 1], flag[k : k + 1], 0)
+        bit = jnp.left_shift(1, iota((32, total), 0))
+        for w in range(cands // 32):
+            bias[ls, 32 * w : 32 * w + 32, :] = jnp.where((words[w : w + 1] & bit) != 0, 0.0, NEG)
 
     scale = 1.0 / math.sqrt(width)
     owned = iota((n, total), 0) == iota((n, total), 1) // slots
-    fold = jnp.concatenate(
-        [hot(iota((total, 128), 1) == part * slots + iota((total, 128), 0) % slots) for part in range(3)],
-        axis=0,
-    )
-
+    fold = [
+        jnp.concatenate(
+            [
+                hot(iota((total, 128), 1) == (3 * ls + part) * slots + iota((total, 128), 0) % slots)
+                for part in range(3)
+            ],
+            axis=0,
+        )
+        for ls in range(own)
+    ]
+
+    whole(recv.at[pl.ds(0, n - 1)], row_sem.at[0], row_sem.at[2]).wait_recv()
+    each_chip(
+        lambda peer: remote(
+            pick.at[peer], recv_pick.at[me], pick_sem.at[0], pick_sem.at[1], peer, 0
+        ).start()
+    )
+    recv_pick[me] = pick[me]
+
+    told = None
     table_copy.wait_recv()
-    whole(recv.at[pl.ds(0, 2 * n - 1)], row_sem.at[0], row_sem.at[1]).wait_recv()
+    whole(recv.at[pl.ds(n, n)], row_sem.at[1], row_sem.at[3]).wait_recv()
     for ls in range(own):
-        scores[...] = dot_nt(
+        scores[ls] = dot_nt(
             jnp.concatenate([desc[own * core + ls], table[ls]], axis=1),
             jnp.concatenate(
                 [recv[x * n : (x + 1) * n, ls].reshape(total, half) for x in range(2)], axis=1
@@ -249,7 +295,7 @@
         def chunk(i, carry):
             top, picked, claimed = carry
             at = pl.ds(pl.multiple_of(i * step, step), step)
-            value = scores[at, :]
+            value = scores[ls, at, :]
             masked = value + bias[ls, at, :]
             claim = jnp.max(masked, axis=1, keepdims=True)
             chosen = code(iota((step, total), 0) + i * step, cands).astype(F32) == picks[ls]
@@ -266,7 +312,7 @@
         start = jnp.full((8, total), NEG, F32)
         top, picked, claimed = [
             jnp.max(v, axis=0, keepdims=True)
-            for v in lax.fori_loop(0, cands // step, chunk, (start, start, start))
+            for v in lax.fori_loop(0, cands // step, chunk, (start, start, start), unroll=True)
         ]
 
         def quality(v):
@@ -281,42 +327,44 @@
             [jnp.where(owned, jnp.broadcast_to(v, (n, total)), 0.0) for v in (high, share - high, top)],
             axis=1,
         ).astype(BF16)
-        res[ls] = dot(spread, fold).reshape(n, 1, 128)
-        each_peer(
-            lambda peer, x: remote(
-                res.at[ls, peer], recv_res.at[ls, x * n + me], res_ss.at[ls], res_rs.at[ls], peer, x
-            ).start()
-        )
-        recv_res[ls, me] = res[ls, me]
+        term = dot(spread, fold[ls])
+        told = term if told is None else told + term
+    res[...] = told.reshape(n, 1, 128)
+    each_peer(
+        lambda peer, x: remote(
+            res.at[peer], recv_res.at[x * n + me], res_sem.at[0], res_sem.at[1], peer, x
+        ).start()
+    )
+    recv_res[me] = res[me]
 
     ones = jnp.ones((128, half), BF16)
     tops = []
-    for ls in range(own):
-        whole(recv_pick.at[ls, pl.ds(0, n - 1)], pick_ss.at[ls], pick_rs.at[ls]).wait_recv()
-        rows = [
-            dot(back[x * own + ls][3], recv_pick[ls, :, x].reshape(total, half)) for x in range(2)
-        ]
-        whole(recv_res.at[ls, pl.ds(0, 2 * n - 1)], res_ss.at[ls], res_rs.at[ls]).wait_recv()
-        for x in range(2):
-            s = own * core_of(x) + ls
-            named, shared, topped, _ = back[x * own + ls]
-            brought = recv_res[ls, x * n : (x + 1) * n].reshape(n, 128).astype(BF16)
-            spread = dot(named, brought)
-            share = dot(jnp.where(shared, spread, 0.0).astype(BF16), ones)
-            phantom[s] = ((1.0 - share) * halo[s].astype(F32) + share * rows[x]).astype(BF16)
-            tops.append(dot_nt(ones[0:8], jnp.where(topped, spread, 0.0).astype(BF16))[0:1])
-    first, second = jnp.concatenate(tops[0::2], axis=0), jnp.concatenate(tops[1::2], axis=0)
+    whole(recv_pick.at[pl.ds(0, n - 1)], pick_sem.at[0], pick_sem.at[1]).wait_recv()
+    rows = [
+        dot(back[x * own + ls][3], recv_pick[:, 2 * ls + x].reshape(total, half)) for x, ls in order
+    ]
+    whole(recv_res.at[pl.ds(0, 2 * n - 1)], res_sem.at[0], res_sem.at[1]).wait_recv()
+    for i, (x, ls) in enumerate(order):
+        s = own * core_of(x) + ls
+        named, shared, topped, _ = back[i]
+        brought = recv_res[x * n : (x + 1) * n].reshape(n, 128).astype(BF16)
+        spread = dot(named, brought)
+        share = dot(jnp.where(shared, spread, 0.0).astype(BF16), ones)
+        phantom[s] = ((1.0 - share) * halo[s].astype(F32) + share * rows[i]).astype(BF16)
+        tops.append(dot_nt(ones[0:8], jnp.where(topped, spread, 0.0).astype(BF16))[0:1])
+    first, second = jnp.concatenate(tops[:own], axis=0), jnp.concatenate(tops[own:], axis=0)
     even = core == 0
     best[...] = jnp.concatenate(
         [jnp.where(even, first, second), jnp.where(even, second, first)], axis=0
     ).astype(BF16)
 
     table_copy.wait_send()
+    whole(send_want.at[pl.ds(0, n - 1)], want_sem.at[0], want_sem.at[1]).wait_send()
     whole(send_meta.at[pl.ds(0, n - 1)], meta_sem.at[0], meta_sem.at[1]).wait_send()
-    whole(send.at[pl.ds(0, 2 * n - 1)], row_sem.at[0], row_sem.at[1]).wait_send()
-    for ls in range(own):
-        whole(pick.at[ls, pl.ds(0, n - 1)], pick_ss.at[ls], pick_rs.at[ls]).wait_send()
-        whole(recv_res.at[ls, pl.ds(0, 2 * n - 1)], res_ss.at[ls], res_rs.at[ls]).wait_send()
+    whole(send.at[pl.ds(0, n - 1)], row_sem.at[0], row_sem.at[2]).wait_send()
+    whole(send.at[pl.ds(0, n)], row_sem.at[1], row_sem.at[3]).wait_send()
+    whole(pick.at[pl.ds(0, n - 1)], pick_sem.at[0], pick_sem.at[1]).wait_send()
+    whole(recv_res.at[pl.ds(0, 2 * n - 1)], res_sem.at[0], res_sem.at[1]).wait_send()
 
 
 def hand_over(phantom_in, best_in, phantom, best):
@@ -350,15 +398,17 @@
             pltpu.VMEM((own, cands, half), BF16),
             pltpu.VMEM((2 * n, own, slots, half), BF16),
             pltpu.VMEM((2 * n, own, slots, half), BF16),
+            pltpu.VMEM((n, 1, 128), F32),
+            pltpu.VMEM((n, 1, 128), F32),
             pltpu.VMEM((n, slots // 2, 128), BF16),
             pltpu.VMEM((n, slots // 2, 128), BF16),
-            pltpu.VMEM((cands, total), F32),
             pltpu.VMEM((own, cands, total), F32),
-            pltpu.VMEM((own, n, 2, slots, half), BF16),
-            pltpu.VMEM((own, n, 2, slots, half), BF16),
-            pltpu.VMEM((own, n, 1, 128), F32),
-            pltpu.VMEM((own, 2 * n, 1, 128), F32),
-            dma((2,)), dma((2,)), dma((own,)), dma((own,)), dma((own,)), dma((own,)), dma((2,)), dma((7,)),
+            pltpu.VMEM((own, cands, total), F32),
+            pltpu.VMEM((n, snaps, slots, half), BF16),
+            pltpu.VMEM((n, snaps, slots, half), BF16),
+            pltpu.VMEM((n, 1, 128), F32),
+            pltpu.VMEM((2 * n, 1, 128), F32),
+            dma((4,)), dma((2,)), dma((2,)), dma((2,)), dma((2,)), dma((2,)), dma((7,)),
         ],
         compiler_params=pltpu.CompilerParams(collective_id=0, has_side_effects=True),
     )(

time: 27.6 us -> 23.9 us (0.87)
  Pallas kernels: 26.7 us -> 23.1 us
    pallas_call x1, Pallas kernels: 26.1 us -> 22.4 us  [body(): pl.pallas_call(functools.partial(kernel, n, slots, 2 * half), out_shape=(...]
where the time goes in v2:
time: 23.9 us; the launch traced here: 23.7 us
  Pallas kernels  23.1 us (97%)
  between operations  0.64 us (3%)
    pallas_call x1, Pallas kernels, body(): pl.pallas_call(functools.partial(kernel, n, slots, 2 * half), out_shape=(...  22.4 us
    pallas_call x1, Pallas kernels, body(): pl.pallas_call(hand_over, out_shape=shapes, in_specs=[pl.BlockSpec(memory...  0.67 us

profile of v2, /device:TPU:0, one launch (start us, length us, event | category | flops | bytes accessed | tf_op | source)
XLA Modules:
  0.0 23.7 jit_solution(3356664874426021608)
XLA Ops:
  0.6 22.4 %shard_map.86 = (bf16[4,128,128]{2,1,0:T(8,128)(2,1)S(1)}, bf16[4,128]{1,0:T(4,128)(2,1)S(1)}) custom-call(bf16[4,128,128]{2,1,0:T(8,128)(2,1)} %halo_in.1, s32[4,128]{1,0:T(4,128)} %unmatched_in.1, s32[4,1,128]{2,1,0:T(1,128)} %bitcast.3, s32[4,16,128]{2,1,0:T(8,128)} %bitcast.2, s32[4,128]{1,0:T(4,128)} %lengths_in.1, s32[4,128]{1,0:T(4,128)} %choice_in.1, ...), custom_call_target="tpu_custom_call" | custom-call | tf_op jit(solution)/shard_map/pallas_call | solution.py:382
  23.0 0.7 %shard_map.87 = (bf16[4,128,128]{2,1,0:T(8,128)(2,1)}, bf16[4,128]{1,0:T(4,128)(2,1)}) custom-call(bf16[4,128,128]{2,1,0:T(8,128)(2,1)S(1)} %get-tuple-element.4.phantom_in, bf16[4,128]{1,0:T(4,128)(2,1)S(1)} %get-tuple-element.5.best_in), custom_call_target="tpu_custom_call" | custom-call | tf_op jit(solution)/shard_map/pallas_call | solution.py:424

commit v3 on v2

--- a/solution.py
+++ b/solution.py
@@ -64,17 +64,21 @@
     def whole(ref, ss, rs):
         return remote(ref, ref, ss, rs, me, 1)
 
-    def each_chip(f):
+    def each_chip(f, part=None):
         if n % 4 or n > 32:
-
-            @pl.loop(1, n)
+            low, high = {None: (1, n), 0: (1, n // 2), 1: (n // 2, n)}[part]
+
+            @pl.loop(low, high)
             def _(d):
                 peer = me + d
                 f(jnp.where(peer >= n, peer - n, peer))
 
             return
+        blocks = [*range(1, n // 4), 0]
+        if part is not None:
+            blocks = blocks[n // 8 :] if part else blocks[: n // 8]
         block, place = me // 4, lax.rem(me, 4)
-        for d in [*range(1, n // 4), 0]:
+        for d in blocks:
             to = block + d
             to = jnp.where(to >= n // 4, to - n // 4, to) * 4
             for q in (3, 1, 2, 0):
@@ -214,8 +218,9 @@
         back.append(
             (
                 hot(iota((halos, n), 1).astype(F32) == dest),
-                (lane == rank + 3 * slots * (i % own)) | (lane == rank + (3 * (i % own) + 1) * slots),
-                lane == rank + (3 * (i % own) + 2) * slots,
+                functools.reduce(
+                    jnp.logical_or, [lane == rank + (3 * (i % own) + part) * slots for part in range(3)]
+                ),
                 hot(iota((halos, total), 1).astype(F32) == target),
             )
         )
@@ -274,11 +279,12 @@
     ]
 
     whole(recv.at[pl.ds(0, n - 1)], row_sem.at[0], row_sem.at[2]).wait_recv()
-    each_chip(
-        lambda peer: remote(
+    def pick_copy(peer):
+        return remote(
             pick.at[peer], recv_pick.at[me], pick_sem.at[0], pick_sem.at[1], peer, 0
-        ).start()
-    )
+        )
+
+    each_chip(lambda peer: pick_copy(peer).start(), 0)
     recv_pick[me] = pick[me]
 
     told = None
@@ -336,22 +342,36 @@
         ).start()
     )
     recv_res[me] = res[me]
-
-    ones = jnp.ones((128, half), BF16)
-    tops = []
+    each_chip(lambda peer: pick_copy(peer).start(), 1)
+
+    kind = iota((128, half + halos), 0) // slots % 3
+    first = iota((128, half + halos), 1) < half
+    merge = hot((first & (kind < 2)) | (~first & (kind == 2)))
+    eye = iota((halos, halos), 0) == iota((halos, halos), 1)
     whole(recv_pick.at[pl.ds(0, n - 1)], pick_sem.at[0], pick_sem.at[1]).wait_recv()
     rows = [
-        dot(back[x * own + ls][3], recv_pick[:, 2 * ls + x].reshape(total, half)) for x, ls in order
+        dot(back[i][2], recv_pick[:, 2 * ls + x].reshape(total, half)) for i, (x, ls) in enumerate(order)
     ]
     whole(recv_res.at[pl.ds(0, 2 * n - 1)], res_sem.at[0], res_sem.at[1]).wait_recv()
+    spread = [
+        dot(
+            jnp.concatenate([back[x * own + ls][0] for ls in range(own)], axis=0),
+            recv_res[x * n : (x + 1) * n].reshape(n, 128).astype(BF16),
+        )
+        for x in range(2)
+    ]
+    spread = jnp.where(
+        jnp.concatenate([v[1] for v in back], axis=0), jnp.concatenate(spread, axis=0), 0.0
+    ).astype(BF16)
+    spread = dot(spread, merge)
+    tops = []
     for i, (x, ls) in enumerate(order):
         s = own * core_of(x) + ls
-        named, shared, topped, _ = back[i]
-        brought = recv_res[x * n : (x + 1) * n].reshape(n, 128).astype(BF16)
-        spread = dot(named, brought)
-        share = dot(jnp.where(shared, spread, 0.0).astype(BF16), ones)
+        share = spread[i * halos : (i + 1) * halos, :half]
         phantom[s] = ((1.0 - share) * halo[s].astype(F32) + share * rows[i]).astype(BF16)
-        tops.append(dot_nt(ones[0:8], jnp.where(topped, spread, 0.0).astype(BF16))[0:1])
+        tops.append(
+            jnp.sum(jnp.where(eye, spread[i * halos : (i + 1) * halos, half:], 0.0), axis=0, keepdims=True)
+        )
     first, second = jnp.concatenate(tops[:own], axis=0), jnp.concatenate(tops[own:], axis=0)
     even = core == 0
     best[...] = jnp.concatenate(

time: 23.9 us -> 23 us (0.962)
  Pallas kernels: 23.1 us -> 22.2 us
    pallas_call x1, Pallas kernels: 22.4 us -> 21.5 us  [body(): pl.pallas_call(functools.partial(kernel, n, slots, 2 * half), out_shape=(...]
where the time goes in v3:
time: 23 us; the launch traced here: 22.8 us
  Pallas kernels  22.2 us (97%)
  between operations  0.64 us (3%)
    pallas_call x1, Pallas kernels, body(): pl.pallas_call(functools.partial(kernel, n, slots, 2 * half), out_shape=(...  21.5 us
    pallas_call x1, Pallas kernels, body(): pl.pallas_call(hand_over, out_shape=shapes, in_specs=[pl.BlockSpec(memory...  0.67 us

profile of v3, /device:TPU:0, one launch (start us, length us, event | category | flops | bytes accessed | tf_op | source)
XLA Modules:
  0.0 22.8 jit_solution(10030004257416316486)
XLA Ops:
  0.6 21.5 %shard_map.86 = (bf16[4,128,128]{2,1,0:T(8,128)(2,1)S(1)}, bf16[4,128]{1,0:T(4,128)(2,1)S(1)}) custom-call(bf16[4,128,128]{2,1,0:T(8,128)(2,1)} %halo_in.1, s32[4,128]{1,0:T(4,128)} %unmatched_in.1, s32[4,1,128]{2,1,0:T(1,128)} %bitcast.3, s32[4,16,128]{2,1,0:T(8,128)} %bitcast.2, s32[4,128]{1,0:T(4,128)} %lengths_in.1, s32[4,128]{1,0:T(4,128)} %choice_in.1, ...), custom_call_target="tpu_custom_call" | custom-call | tf_op jit(solution)/shard_map/pallas_call | solution.py:402
  22.2 0.7 %shard_map.87 = (bf16[4,128,128]{2,1,0:T(8,128)(2,1)}, bf16[4,128]{1,0:T(4,128)(2,1)}) custom-call(bf16[4,128,128]{2,1,0:T(8,128)(2,1)S(1)} %get-tuple-element.4.phantom_in, bf16[4,128]{1,0:T(4,128)(2,1)S(1)} %get-tuple-element.5.best_in), custom_call_target="tpu_custom_call" | custom-call | tf_op jit(solution)/shard_map/pallas_call | solution.py:444

commit v4 on v3

--- a/solution.py
+++ b/solution.py
@@ -12,7 +12,7 @@
 F32 = jnp.float32
 BF16 = jnp.bfloat16
 NEG = -1e30
-GROUP = 32
+PARTS = 4
 NT = (((1,), (1,)), ((), ()))
 
 
@@ -50,7 +50,7 @@
     cands = desc.shape[1]
     own = snaps // 2
     total = n * slots
-    hs = slots // 2
+    qs = slots // PARTS
 
     def core_of(x):
         return 1 - core if x else core
@@ -149,31 +149,26 @@
 
     blocks, rows = [], []
     for ls in range(own):
-        s = own * core + ls
         dest, rank, _, live = route[ls]
-        listed = jnp.where(k_ids < lengths[pl.ds(s, 1), :], coded[ls], 0)
-        taken = jnp.sum(jnp.where(k_ids == choice[pl.ds(s, 1), :], coded[ls], 0), axis=0, keepdims=True)
-        parts = [listed, jnp.broadcast_to(taken, (GROUP - k_count, halos))]
-        parts = [jnp.zeros((GROUP * ls, halos), jnp.int32)] * (ls > 0) + parts
-        if ls < own - 1:
-            parts.append(jnp.zeros((GROUP * (own - 1 - ls), halos), jnp.int32))
-        blocks.append(jnp.concatenate(parts, axis=0).astype(F32).astype(BF16))
+        listed = jnp.where(k_ids < lengths[pl.ds(own * core + ls, 1), :], coded[ls], 0).astype(F32)
+        none = jnp.zeros((k_count, halos), F32)
+        blocks.append(jnp.concatenate([listed if i == ls else none for i in range(own)], axis=0))
         rows.append(
             [
-                jnp.where(live & (rank >= g * hs) & (rank < (g + 1) * hs), dest * hs + rank - g * hs, -1)
-                for g in range(2)
+                jnp.where(live & (rank >= g * qs) & (rank < (g + 1) * qs), dest * qs + rank - g * qs, -1)
+                for g in range(PARTS)
             ]
         )
-    block = jnp.concatenate(blocks, axis=1)
+    block = jnp.concatenate(blocks, axis=1).astype(BF16)
     blank = jnp.zeros_like(block)
     meta = sum(
         dot_nt(
-            jnp.concatenate([hot(iota((n * hs, halos), 0) == r[g]) for r in rows], axis=1),
-            jnp.concatenate([blank, block] if g else [block, blank], axis=0),
-        )
-        for g in range(2)
-    )
-    send_meta[...] = meta.astype(BF16).reshape(n, hs, 128)
+            jnp.concatenate([hot(iota((n * qs, halos), 0) == r[g]) for r in rows], axis=1),
+            jnp.concatenate([block if i == g else blank for i in range(PARTS)], axis=0),
+        )
+        for g in range(PARTS)
+    )
+    send_meta[...] = meta.astype(BF16).reshape(n, qs, 128)
 
     loads[5].wait()
     for i, (x, ls) in enumerate(order):
@@ -224,11 +219,11 @@
                 hot(iota((halos, total), 1).astype(F32) == target),
             )
         )
-    entry = iota((n * hs, total), 0)
-    column = iota((n * hs, total), 1)
+    entry = iota((n * qs, total), 0)
+    column = iota((n * qs, total), 1)
     inside = column % slots
     unpack = [
-        hot((entry == (column // slots) * hs + inside - g * hs) & (inside // hs == g)) for g in range(2)
+        hot((entry == (column // slots) * qs + inside - g * qs) & (inside // qs == g)) for g in range(PARTS)
     ]
     loads[6].wait()
 
@@ -240,21 +235,20 @@
     whole(recv_want.at[pl.ds(0, n - 1)], want_sem.at[0], want_sem.at[1]).wait_recv()
     wanted = dot(from_chip, recv_want[...].reshape(n, 128).astype(BF16))
     wanted = jnp.where(its_slot, wanted, 0.0).astype(BF16)
+    picks = dot_nt(hot(iota((8, 128), 1) // slots == iota((8, 128), 0)), wanted)
     for i, (x, ls) in enumerate(order):
         at = jnp.concatenate([dot(wanted, part[i])] * (cands // 128), axis=1)
         chosen = dot(hot(at == ids), desc[own * core_of(x) + ls]).astype(BF16)
         pick[:, 2 * ls + x] = chosen.reshape(n, slots, half)
     step = 64
     whole(recv_meta.at[pl.ds(0, n - 1)], meta_sem.at[0], meta_sem.at[1]).wait_recv()
-    arrived = recv_meta[...].reshape(n * hs, 128).astype(F32).T.astype(BF16)
-    picks = []
+    arrived = recv_meta[...].reshape(n * qs, 128).astype(F32).T.astype(BF16)
     for ls in range(own):
         lists = sum(
-            dot(arrived[(g * own + ls) * GROUP : (g * own + ls + 1) * GROUP], unpack[g]) for g in range(2)
-        )
-        picks.append(lists[k_count : k_count + 1])
-
-        listed = lists[:k_count].astype(jnp.int32)
+            dot(arrived[(g * own + ls) * k_count : (g * own + ls + 1) * k_count], unpack[g])
+            for g in range(PARTS)
+        )
+        listed = lists.astype(jnp.int32)
         at = listed + cands // 2 - jnp.where(listed > 0, 1, 0)
         flag = jnp.where(listed == 0, 0, jnp.left_shift(1, at & 31))
         at = at >> 5
@@ -304,7 +298,7 @@
             value = scores[ls, at, :]
             masked = value + bias[ls, at, :]
             claim = jnp.max(masked, axis=1, keepdims=True)
-            chosen = code(iota((step, total), 0) + i * step, cands).astype(F32) == picks[ls]
+            chosen = code(iota((step, total), 0) + i * step, cands).astype(F32) == picks[ls : ls + 1]
 
             def least(v):
                 return jnp.max(v.reshape(step // 8, 8, total), axis=0)
@@ -420,8 +414,8 @@
             pltpu.VMEM((2 * n, own, slots, half), BF16),
             pltpu.VMEM((n, 1, 128), F32),
             pltpu.VMEM((n, 1, 128), F32),
-            pltpu.VMEM((n, slots // 2, 128), BF16),
-            pltpu.VMEM((n, slots // 2, 128), BF16),
+            pltpu.VMEM((n, slots // PARTS, 128), BF16),
+            pltpu.VMEM((n, slots // PARTS, 128), BF16),
             pltpu.VMEM((own, cands, total), F32),
             pltpu.VMEM((own, cands, total), F32),
             pltpu.VMEM((n, snaps, slots, half), BF16),

time: 23 us -> 22.6 us (0.983)
  Pallas kernels: 22.2 us -> 21.8 us
    pallas_call x1, Pallas kernels: 21.5 us -> 21.1 us  [body(): pl.pallas_call(functools.partial(kernel, n, slots, 2 * half), out_shape=(...]
where the time goes in v4:
time: 22.6 us; the launch traced here: 22.4 us
  Pallas kernels  21.8 us (96%)
  between operations  0.64 us (3%)
    pallas_call x1, Pallas kernels, body(): pl.pallas_call(functools.partial(kernel, n, slots, 2 * half), out_shape=(...  21.1 us
    pallas_call x1, Pallas kernels, body(): pl.pallas_call(hand_over, out_shape=shapes, in_specs=[pl.BlockSpec(memory...  0.67 us

profile of v4, /device:TPU:0, one launch (start us, length us, event | category | flops | bytes accessed | tf_op | source)
XLA Modules:
  0.0 22.4 jit_solution(10599482411204790765)
XLA Ops:
  0.6 21.1 %shard_map.86 = (bf16[4,128,128]{2,1,0:T(8,128)(2,1)S(1)}, bf16[4,128]{1,0:T(4,128)(2,1)S(1)}) custom-call(bf16[4,128,128]{2,1,0:T(8,128)(2,1)} %halo_in.1, s32[4,128]{1,0:T(4,128)} %unmatched_in.1, s32[4,1,128]{2,1,0:T(1,128)} %bitcast.3, s32[4,16,128]{2,1,0:T(8,128)} %bitcast.2, s32[4,128]{1,0:T(4,128)} %lengths_in.1, s32[4,128]{1,0:T(4,128)} %choice_in.1, ...), custom_call_target="tpu_custom_call" | custom-call | tf_op jit(solution)/shard_map/pallas_call | solution.py:396
  21.8 0.7 %shard_map.87 = (bf16[4,128,128]{2,1,0:T(8,128)(2,1)}, bf16[4,128]{1,0:T(4,128)(2,1)}) custom-call(bf16[4,128,128]{2,1,0:T(8,128)(2,1)S(1)} %get-tuple-element.4.phantom_in, bf16[4,128]{1,0:T(4,128)(2,1)S(1)} %get-tuple-element.5.best_in), custom_call_target="tpu_custom_call" | custom-call | tf_op jit(solution)/shard_map/pallas_call | solution.py:438
